TPU v7x, 16 devices: a 4x2x1 block of a 4x4x8 slice. The times are simulated.
16 devices in a mesh: dp: 2 (over y, z), tp: 8 (over x, core).
Axes of the slice: x: 4, y: 2, z: 1, core: 2. Of those that a mesh axis runs over, the one named last changes fastest.
The devices are a block of a 4x4x8 slice.
Arguments:
- x: bfloat16 [8192, 2048], P(('dp', 'tp')), parts along dimension 0
- dy: bfloat16 [8192, 2048], P(('dp', 'tp')), parts along dimension 0
- gate: bfloat16 [8192, 16384], P('dp', 'tp'), parts along dimension 0
- up: bfloat16 [8192, 16384], P('dp', 'tp'), parts along dimension 0
- w_gate: bfloat16 [2048, 16384], P(None, 'tp')
- w_up: bfloat16 [2048, 16384], P(None, 'tp')
- w_down: bfloat16 [16384, 2048], P('tp')
Outputs:
- output 1: bfloat16 [8192, 2048], P(('dp', 'tp')), parts along dimension 0
- output 2: bfloat16 [4096, 16384], P('dp', 'tp'), parts along dimension 0
- output 3: bfloat16 [4096, 16384], P('dp', 'tp'), parts along dimension 0
- output 4: bfloat16 [32768, 2048], P(('dp', 'tp')), parts along dimension 0
There are 2 independent parts. A program takes and returns all parts, laid end to end along the dimension named above; an argument that names none is the same for every part.
All inputs are finite; a program needn't handle non-finite values.
Results may differ from a plain program's by a relative error of at most 0.012.
Values are sent between devices in bfloat16 or wider.
A program may use at most 768 MiB of HBM per device.

v0:
```python
import jax
import jax.numpy as jnp


def act(gate, up):
    return jax.nn.gelu(gate) * up


def solution(mesh):
    def step(x, dy, gate, up, w_gate, w_up, w_down):
        hidden, back = jax.vjp(act, gate.astype(jnp.float32), up.astype(jnp.float32))
        d_hidden = jnp.dot(dy, w_down.T, preferred_element_type=jnp.float32)
        d_gate, d_up = (g.astype(jnp.bfloat16) for g in back(d_hidden))
        dx = jnp.dot(d_gate, w_gate.T) + jnp.dot(d_up, w_up.T)
        groups = mesh.shape["dp"]

        def by_group(a, b):
            a, b = (t.reshape(groups, -1, t.shape[-1]) for t in (a, b))
            product = jnp.einsum("gta,gtb->gab", a, b, preferred_element_type=jnp.float32)
            return product.astype(jnp.bfloat16).reshape(-1, b.shape[-1])

        return dx, by_group(x, d_gate), by_group(x, d_up), by_group(hidden.astype(jnp.bfloat16), dy)

    return step
```

profile of v0, /device:TPU:112, one launch (start us, length us, event | category | flops | bytes accessed | tf_op | source)
XLA Modules:
  0.0 434.7 jit_solution(11651592163767289366)
XLA Ops:
  7.2 0.1 all-gather.11.cloned.1.call-start
  7.2 0.7 all-gather.11.cloned.1.call-update
  8.0 0.1 all-gather.13.cloned.1.call-start
  8.0 0.7 all-gather.13.cloned.1.call-update
  8.8 0.1 reduce-scatter.4.cloned.1.call-start
  8.9 84.7 %all-gather.11.cloned.1.call-done = bf16[4096,2048]{1,0:T(8,128)(2,1)} async-done(((bf16[512,2048]{1,0:T(8,128)(2,1)}), bf16[4096,2048]{1,0:T(8,128)(2,1)}) %all-gather.11.cloned.1.call-update) | async-done | bytes 16777232 | tf_op args[1]
  93.6 65.4 %fusion.4 = (bf16[4096,2048]{1,0:T(8,128)(2,1)}, f32[4096,2048]{1,0:T(8,128)}) fusion(bf16[4096,2048]{1,0:T(8,128)(2,1)} %param.3, bf16[4096,2048]{1,0:T(8,128)(2,1)} %param.2, bf16[4096,2048]{1,0:T(8,128)(2,1)} %all-gather.11.cloned.1.call-done, bf16[2048,2048]{1,0:T(8,128)(2,1)} %param.1), kind=kOutput, calls=%fused_computation.11 | convolution fusion | flops 34552676352 | bytes 109051904 | tf_op jit(solution)/dot_general | solution.py:12
  159.0 42.5 %fusion.19 = bf16[4096,2048]{1,0:T(8,128)(2,1)} fusion(bf16[4096,2048]{1,0:T(8,128)(2,1)} %get-tuple-element.4, bf16[2048,2048]{1,0:T(8,128)(2,1)} %param.4), kind=kOutput, calls=%fused_computation.27 | convolution fusion | flops 34359738368 | bytes 41943040 | tf_op jit(solution)/dot_general | solution.py:14
  201.4 48.8 %convolution_add_fusion = bf16[4096,2048]{1,0:T(8,128)(2,1)} fusion(bf16[4096,2048]{1,0:T(8,128)(2,1)} %fusion.19, bf16[2048,2048]{1,0:T(8,128)(2,1)} %param.5, f32[4096,2048]{1,0:T(8,128)} %get-tuple-element.5, bf16[4096,2048]{1,0:T(8,128)(2,1)} %param.3), kind=kOutput, calls=%fused_computation.19 | convolution fusion | flops 34460401664 | bytes 92274688 | tf_op jit(solution)/dot_general | solution.py:14
  250.3 0.1 reduce-scatter.4.cloned.1.call-update
  250.3 0.0 all-gather.13.cloned.1.call-done
  250.4 54.5 %convert_bitcast_fusion = bf16[2048,2048]{0,1:T(8,128)(2,1)} fusion(bf16[4096,2048]{1,0:T(8,128)(2,1)} %all-gather.13.cloned.1.call-done, f32[4096,2048]{1,0:T(8,128)} %get-tuple-element.5, bf16[4096,2048]{1,0:T(8,128)(2,1)} %param.3), kind=kOutput, calls=%fused_computation.20 | convolution fusion | flops 34456207360 | bytes 75497472 | tf_op jit(solution)/gta,gtb->gab/dot_general | solution.py:19
  304.9 12.2 %copy.1 = bf16[2048,2048]{1,0:T(8,128)(2,1)} copy(bf16[2048,2048]{0,1:T(8,128)(2,1)} %convert_bitcast_fusion) | data formatting | bytes 16777216
  317.1 43.5 %convert_bitcast_fusion.1 = bf16[2048,2048]{0,1:T(8,128)(2,1)} fusion(bf16[4096,2048]{1,0:T(8,128)(2,1)} %get-tuple-element.4, bf16[4096,2048]{1,0:T(8,128)(2,1)} %all-gather.13.cloned.1.call-done), kind=kOutput, calls=%fused_computation.21 | convolution fusion | flops 34363932672 | bytes 41943040 | tf_op jit(solution)/gta,gtb->gab/dot_general | solution.py:19
  360.5 12.2 %copy = bf16[2048,2048]{1,0:T(8,128)(2,1)} copy(bf16[2048,2048]{0,1:T(8,128)(2,1)} %convert_bitcast_fusion.1) | data formatting | bytes 16777216
  372.8 55.0 %fusion.12 = bf16[2048,2048]{1,0:T(8,128)(2,1)} fusion(bf16[4096,2048]{1,0:T(8,128)(2,1)} %all-gather.11.cloned.1.call-done, bf16[4096,2048]{1,0:T(8,128)(2,1)} %param.2, bf16[4096,2048]{1,0:T(8,128)(2,1)} %param.3), kind=kOutput, calls=%fused_computation.22 | convolution fusion | flops 34464595968 | bytes 58720256 | tf_op jit(solution)/gta,gtb->gab/dot_general | solution.py:19
  427.7 0.0 reduce-scatter.4.cloned.1.call-done
Async XLA Ops:
  7.2 86.4 %all-gather.11.cloned.1.call-start = ((), (), s32[]{:S(2)}) async-start(), calls=%async_computation.1 | async-start | bytes 18874368 | tf_op args[1]
  8.0 242.4 %all-gather.13.cloned.1.call-start = ((), (), s32[]{:S(2)}) async-start(), calls=%async_computation.2 | async-start | bytes 18874368 | tf_op jit(solution)/reshape | solution.py:18
  8.8 418.9 %reduce-scatter.4.cloned.1.call-start = ((), (), s32[]{:S(2)}) async-start(), calls=%async_computation.3 | async-start | bytes 18874368
Sparse Core Ops, SparseCore 0:
  9.6 83.9 all-gather.10
  95.2 81.6 all-gather.12
  250.4 88.2 reduce-scatter.3
where the time goes:
time: 442 us; the launch traced here: 435 us
  matrix products  310 us (70%)
  waiting for transfers between devices  86.3 us (20%)
  local copies, waits for them, and re-layouts  24.5 us (6%)
  between operations  14.2 us (3%)
    dot_general x3, matrix products, by_group(): jnp.einsum('gta,gtb->gab', a, b, preferred_element_type=jnp.float32)  153 us
    dot_general x2, matrix products, step(): dx = jnp.dot(d_gate, w_gate.T) + jnp.dot(d_up, w_up.T)  91.3 us
    unnamed x5, waiting for transfers between devices  86.2 us
    dot_general x1, matrix products, step(): d_hidden = jnp.dot(dy, w_down.T, preferred_element_type=jnp.float32)  65.4 us
    unnamed x2, local copies, waits for them, and re-layouts  24.5 us
  transfers between devices with their start and end apart: 3, of which 1 were waited for; matrix products, arithmetic and copies ran while one was open for 77% of the time, Pallas kernels for 0%

commit v1 on v0

v1 whole, which is shorter than its diff:
```python
import functools

import jax
import jax.numpy as jnp
from jax import lax
from jax.experimental import pallas as pl
from jax.experimental.pallas import tpu as pltpu
from jax.sharding import PartitionSpec as P

MESH = pl.DeviceIdType.MESH
VMEM_LIMIT = 63 * 2**20
TM = 256
F32, BF16 = jnp.float32, jnp.bfloat16
NT = (((1,), (1,)), ((), ()))
TN = (((0,), (0,)), ((), ()))
ROOT = 0.7978845608028654


def place(i):
    a = i // 4
    mid, far = ((a + 1) // 2) % 2, a // 3
    chip = mid * (2 * (i % 2) - 1) + 2 * far
    half = mid * ((a - 1 + i % 2) % 2) + (1 - mid) * (i % 2)
    return chip, (i // 2) % 2, half


def row_block(i, chips):
    t = lax.axis_index("tp")
    chip, core, half = place(i)
    return ((((t // 2) + chip + chips) % chips) * 2 + (t % 2 + core) % 2) * 2 + half


def backward_act(dh, g, u):
    g2 = g * g
    t = jnp.tanh(ROOT * (g * (1.0 + 0.044715 * g2)))
    cdf = 0.5 + 0.5 * t
    act = g * cdf
    slope = cdf + (0.5 * ROOT) * g * ((1.0 - t * t) * (1.0 + (3 * 0.044715) * g2))
    return act * u, dh * u * slope, dh * act


def kernel_a(chips, dy_ref, x_ref, g_ref, u_ref, wd_ref, wg_ref, wu_ref,
             yx_ref, act_ref, own_ref, other_ref,
             wd, wgu, dybuf, dh, sbuf, w_sem, ld_sem, cp_sem, sdy, rdy, sx, rx, so, ro):
    i = pl.program_id(0)
    steps = pl.num_programs(0)
    t = lax.axis_index("tp")
    n = 2 * chips
    partner = t + 1 - 2 * (t % 2)
    right, left = (t + 2) % n, (t + n - 2) % n
    dp = lax.axis_index("dp")
    ff = wd.shape[0]
    tokens = yx_ref.shape[0] // 2
    dyf_ref, xf_ref = yx_ref.at[pl.ds(0, tokens)], yx_ref.at[pl.ds(tokens, tokens)]

    def tile(ref, j):
        return ref.at[pl.ds(j * TM, TM)]

    def send(src, full, j, to, ssem, rsem):
        return pltpu.make_async_remote_copy(src_ref=src, dst_ref=tile(full, j), send_sem=ssem.at[j], recv_sem=rsem.at[j],
                                            device_id=(dp, to), device_id_type=MESH)

    def arrived(full, j, ssem, rsem):
        send(tile(full, j), full, j, partner, ssem, rsem).wait_recv()

    def hand_over(j):
        k = (j // 4) * 2 + j % 2
        return send(sbuf.at[j % 2], other_ref, k, partner, so, ro)

    def load(src, slot):
        return pltpu.make_async_copy(src, dybuf.at[slot], ld_sem.at[slot])

    w_copies = [
        pltpu.make_async_copy(wd_ref, wd, w_sem.at[0]),
        pltpu.make_async_copy(wg_ref, wgu.at[:, pl.ds(0, ff)], w_sem.at[1]),
        pltpu.make_async_copy(wu_ref, wgu.at[:, pl.ds(ff, ff)], w_sem.at[2]),
    ]
    own_copies = [
        pltpu.make_async_copy(dy_ref, dyf_ref.at[pl.ds(0, 2 * TM)], cp_sem.at[0]),
        pltpu.make_async_copy(x_ref, xf_ref.at[pl.ds(0, 2 * TM)], cp_sem.at[1]),
    ]

    def ring(src, full, ssem, rsem):
        send(tile(src, 0), full, 4, right, ssem, rsem).start()
        send(tile(src, 1), full, 5, left, ssem, rsem).start()
        send(tile(src, 1), full, 8, right, ssem, rsem).start()
        send(tile(src, 0), full, 9, left, ssem, rsem).start()

    def pair(src, full, ssem, rsem):
        send(tile(src, 0), full, 2, partner, ssem, rsem).start()
        send(tile(src, 1), full, 3, partner, ssem, rsem).start()

    @pl.when(i == 0)
    def _():
        w_copies[0].start()
        load(tile(dy_ref, 0), 0).start()
        w_copies[1].start()
        w_copies[2].start()
        barrier = pltpu.get_barrier_semaphore()
        for other in (partner, left, right):
            pl.semaphore_signal(barrier, inc=1, device_id=(dp, other), device_id_type=MESH)
        pl.semaphore_wait(barrier, 3)
        pair(dy_ref, dyf_ref, sdy, rdy)
        ring(dy_ref, dyf_ref, sdy, rdy)
        load(tile(dy_ref, 1), 1).start()
        pair(x_ref, xf_ref, sx, rx)
        for c in own_copies:
            c.start()

    j = i + 1

    @pl.when((j >= 2) & (j < steps))
    def _():
        arrived(dyf_ref, j, sdy, rdy)
        load(tile(dyf_ref, j), j % 2).start()

        @pl.when((j >= 4) & (j % 4 < 2))
        def _():
            send(tile(dyf_ref, j), dyf_ref, j + 2, partner, sdy, rdy).start()

        @pl.when(j == 4)
        def _():
            send(tile(dyf_ref, 4), dyf_ref, 12, right, sdy, rdy).start()

        @pl.when(j == 5)
        def _():
            send(tile(dyf_ref, 5), dyf_ref, 13, left, sdy, rdy).start()

    @pl.when(i == 6)
    def _():
        ring(x_ref, xf_ref, sx, rx)

    @pl.when(i == 12)
    def _():
        for k in (4, 5):
            arrived(xf_ref, k, sx, rx)
            send(tile(xf_ref, k), xf_ref, k + 2, partner, sx, rx).start()
        send(tile(xf_ref, 4), xf_ref, 12, right, sx, rx).start()
        send(tile(xf_ref, 5), xf_ref, 13, left, sx, rx).start()

    @pl.when(i == 15)
    def _():
        for k in (8, 9):
            arrived(xf_ref, k, sx, rx)
            send(tile(xf_ref, k), xf_ref, k + 2, partner, sx, rx).start()

    @pl.when((i >= 3) & ((i - 1) % 4 >= 2))
    def _():
        hand_over(i - 1).start()

    @pl.when((i >= 4) & (i % 4 >= 2))
    def _():
        hand_over(i - 4).wait_send()

    slot = i % 2
    load(tile(dy_ref, 0), slot).wait()

    @pl.when(i == 0)
    def _():
        w_copies[0].wait()

    CB = 256
    for c in range(ff // CB):
        cols = pl.ds(c * CB, CB)
        dh[c % 2] = lax.dot_general(dybuf[slot], wd[cols, :], NT, preferred_element_type=F32)
        for r in range(TM // 32):
            rows = pl.ds(r * 32, 32)
            h, dg, du = backward_act(dh[c % 2, rows, :], g_ref[rows, cols].astype(F32), u_ref[rows, cols].astype(F32))
            act_ref[rows, cols] = h.astype(BF16)
            act_ref[rows, pl.ds(ff + c * CB, CB)] = dg.astype(BF16)
            act_ref[rows, pl.ds(2 * ff + c * CB, CB)] = du.astype(BF16)

    @pl.when(i == 0)
    def _():
        w_copies[1].wait()
        w_copies[2].wait()

    def term(put):
        d = wgu.shape[0]
        NB = 512
        for c in range(d // NB):
            cols = pl.ds(c * NB, NB)
            put(cols, lax.dot_general(act_ref[:, pl.ds(ff, 2 * ff)], wgu[cols, :], NT, preferred_element_type=F32))

    @pl.when(i % 4 < 2)
    def _():
        def put(cols, v):
            own_ref[:, cols] = v
        term(put)

    @pl.when(i % 4 >= 2)
    def _():
        def put(cols, v):
            sbuf[i % 2, :, cols] = v.astype(BF16)
        term(put)

    @pl.when(i == steps - 1)
    def _():
        for k in (12, 13):
            arrived(xf_ref, k, sx, rx)
            send(tile(xf_ref, k), xf_ref, k + 2, partner, sx, rx).start()
        for k in (2, 3, 6, 7, 10, 11, 14, 15):
            arrived(xf_ref, k, sx, rx)
        for k in range(2, 16):
            send(tile(dy_ref, 0), dyf_ref, k, partner, sdy, rdy).wait_send()
            send(tile(x_ref, 0), xf_ref, k, partner, sx, rx).wait_send()
        for c in own_copies:
            c.wait()
        last = hand_over(tokens // TM - 1)
        last.start()
        for k in range(tokens // TM // 2):
            send(sbuf.at[0], other_ref, k, partner, so, ro).wait_recv()
        hand_over(tokens // TM - 2).wait_send()
        last.wait_send()


def call_a(chips, dy, x, gate, up, wd, wg, wu):
    rows, ff = gate.shape
    d = dy.shape[1]
    any_ = pl.BlockSpec(memory_space=pl.ANY)
    kept = pl.BlockSpec((TM, ff), lambda i: (row_block(i, chips), 0))
    return pl.pallas_call(
        functools.partial(kernel_a, chips),
        grid=(rows // TM,),
        in_specs=[any_, any_, kept, kept, any_, any_, any_],
        out_specs=[
            any_,
            pl.BlockSpec((TM, 3 * ff), lambda i: (i, 0)),
            pl.BlockSpec((TM, d), lambda i: ((i // 4) * 2 + (i % 4 + 2) // 3, 0)),
            any_,
        ],
        out_shape=[
            jax.ShapeDtypeStruct((2 * rows, d), BF16), jax.ShapeDtypeStruct((rows, 3 * ff), BF16),
            jax.ShapeDtypeStruct((rows // 2, d), F32), jax.ShapeDtypeStruct((rows // 2, d), BF16),
        ],
        scratch_shapes=[
            pltpu.VMEM((ff, d), BF16), pltpu.VMEM((d, 2 * ff), BF16),
            pltpu.VMEM((2, TM, d), BF16), pltpu.VMEM((2, TM, 256), F32), pltpu.VMEM((2, TM, d), BF16),
            pltpu.SemaphoreType.DMA((3,)), pltpu.SemaphoreType.DMA((2,)), pltpu.SemaphoreType.DMA((2,)),
            pltpu.SemaphoreType.DMA((16,)), pltpu.SemaphoreType.DMA((16,)),
            pltpu.SemaphoreType.DMA((16,)), pltpu.SemaphoreType.DMA((16,)),
            pltpu.SemaphoreType.DMA((8,)), pltpu.SemaphoreType.DMA((8,)),
        ],
        compiler_params=pltpu.CompilerParams(collective_id=0, has_side_effects=True, vmem_limit_bytes=VMEM_LIMIT,
                                             dimension_semantics=("arbitrary",)),
        cost_estimate=pl.CostEstimate(flops=6 * rows * d * ff, bytes_accessed=12 * rows * d, transcendentals=rows * ff),
        name="gather_and_dx",
    )(dy, x, gate, up, wd, wg, wu)


SUB = TM // 2
HOPS = ((2, 3), (6, 7), (5, 4), (0, 1))
EVENTS = [(h, q) for h in range(4) for q in range(2)]
POINTS = (0, 0, 3, 6, 8, 10, 13, 15)


def kernel_b(chips, a_ref, b_ref, own_ref, other_ref, w_ref, dx_ref,
             own, other, come, go, ld_sem, s_sem, r_sem, o_sem):
    s = pl.program_id(0)
    t = lax.axis_index("tp")
    n = 2 * chips
    dp = lax.axis_index("dp")
    ways = ((t + 2) % n, (t + n - 2) % n)

    def loads(e):
        h, q = EVENTS[e]
        for w in range(2):
            at = pl.ds(HOPS[h][w] * TM + q * SUB, SUB)
            yield pltpu.make_async_copy(own_ref.at[at], own.at[e % 2, w], ld_sem.at[e % 2, w, 0])
            yield pltpu.make_async_copy(other_ref.at[at], other.at[e % 2, w], ld_sem.at[e % 2, w, 1])

    def send(e, w):
        return pltpu.make_async_remote_copy(src_ref=go.at[e % 2, w], dst_ref=come.at[e, w], send_sem=s_sem.at[e, w],
                                            recv_sem=r_sem.at[e, w], device_id=(dp, ways[w]), device_id_type=MESH)

    def finish(e, w):
        q = EVENTS[e][1]
        return pltpu.make_async_copy(go.at[e % 2, w], dx_ref.at[pl.ds(w * TM + q * SUB, SUB)], o_sem.at[q, w])

    def event(e):
        h = EVENTS[e][0]
        if e == 0:
            barrier = pltpu.get_barrier_semaphore()
            for c in loads(0):
                c.start()
            for other_ in ways:
                pl.semaphore_signal(barrier, inc=1, device_id=(dp, other_), device_id_type=MESH)
            pl.semaphore_wait(barrier, 2)
        if e + 1 < len(EVENTS):
            for c in loads(e + 1):
                c.start()
        for c in loads(e):
            c.wait()
        for w in range(2):
            if e >= 2:
                send(e - 2, w).wait_recv()
                send(e - 2, w).wait_send()

            @pl.loop(0, SUB // 16)
            def _(r):
                rows = pl.ds(pl.multiple_of(r * 16, 16), 16)
                v = own[e % 2, w, rows, :] + other[e % 2, w, rows, :].astype(F32)
                if e >= 2:
                    v = v + come[e - 2, w, rows, :].astype(F32)
                go[e % 2, w, rows, :] = v.astype(BF16)
        for w in range(2):
            if h < 3:
                send(e, w).start()
            else:
                finish(e, w).start()

    def at_point(half):
        for e, p in enumerate(POINTS):
            if p % 2 == half:
                @pl.when(s == p // 2)
                def _(e=e):
                    event(e)

    for half in range(2):
        at_point(half)

        @pl.when(s < 4)
        def _():
            cols = pl.ds(half * 512, 512)
            w_ref[:, cols] = lax.dot_general(a_ref[...], b_ref[:, cols], TN, preferred_element_type=F32).astype(BF16)

        @pl.when(s >= 4)
        def _():
            cols = pl.ds(half * 512, 512)
            w_ref[:, cols] = lax.dot_general(b_ref[...], a_ref[:, cols], TN, preferred_element_type=F32).astype(BF16)

    @pl.when(s == pl.num_programs(0) - 1)
    def _():
        for e in (6, 7):
            for w in range(2):
                finish(e, w).wait()


def call_b(chips, act, yx, own, other):
    rows, d = act.shape[0], yx.shape[1]
    ff = act.shape[1] // 3
    any_ = pl.BlockSpec(memory_space=pl.ANY)
    q = lambda s: s // 4
    return pl.pallas_call(
        functools.partial(kernel_b, chips),
        grid=(8,),
        in_specs=[
            pl.BlockSpec((rows, ff // 2), lambda s: (0, s // 2)),
            pl.BlockSpec((rows, d // 2), lambda s: (q(s), s % 2)),
            any_, any_,
        ],
        out_specs=[
            pl.BlockSpec((ff // 2, d // 2), lambda s: ((1 - q(s)) * (s // 2) + q(s) * (2 + s % 2), (1 - q(s)) * (s % 2) + q(s) * (s // 2 - 2))),
            any_,
        ],
        out_shape=[jax.ShapeDtypeStruct((ff + d, d), BF16), jax.ShapeDtypeStruct((2 * TM, d), BF16)],
        scratch_shapes=[
            pltpu.VMEM((2, 2, SUB, d), F32), pltpu.VMEM((2, 2, SUB, d), BF16),
            pltpu.VMEM((6, 2, SUB, d), BF16), pltpu.VMEM((2, 2, SUB, d), BF16),
            pltpu.SemaphoreType.DMA((2, 2, 2)), pltpu.SemaphoreType.DMA((6, 2)), pltpu.SemaphoreType.DMA((6, 2)),
            pltpu.SemaphoreType.DMA((2, 2)),
        ],
        compiler_params=pltpu.CompilerParams(collective_id=1, has_side_effects=True, vmem_limit_bytes=VMEM_LIMIT,
                                             dimension_semantics=("arbitrary",)),
        cost_estimate=pl.CostEstimate(flops=4 * rows * d * ff, bytes_accessed=12 * rows * d, transcendentals=0),
        name="scatter_and_dw",
    )(act, yx, own, other)


def call_c(act, yx, w, dx):
    rows, d = act.shape[0], yx.shape[1]
    ff = act.shape[1] // 3

    def kernel(x_ref, du_ref, wd_ref, wg_ref, dx_ref, dx_out, wg_out, wu_out, wd_out):
        for half in range(2):
            cols = pl.ds(half * 512, 512)
            wu_out[:, cols] = lax.dot_general(x_ref[...], du_ref[:, cols], TN, preferred_element_type=F32).astype(BF16)
        dx_out[...] = dx_ref[...]
        wg_out[...] = wg_ref[...]
        wd_out[...] = wd_ref[...]

    return pl.pallas_call(
        kernel,
        grid=(4,),
        in_specs=[
            pl.BlockSpec((rows, d // 2), lambda s: (1, s % 2)),
            pl.BlockSpec((rows, ff // 2), lambda s: (0, 4 + s // 2)),
            pl.BlockSpec((ff // 4, d), lambda s: (s, 0)),
            pl.BlockSpec((d // 4, d), lambda s: (4 + s, 0)),
            pl.BlockSpec((dx.shape[0] // 4, d), lambda s: (s, 0)),
        ],
        out_specs=[
            pl.BlockSpec((dx.shape[0] // 4, d), lambda s: (s, 0)),
            pl.BlockSpec((d // 4, d), lambda s: (s, 0)),
            pl.BlockSpec((d // 2, ff // 2), lambda s: (s % 2, s // 2)),
            pl.BlockSpec((ff // 4, d), lambda s: (s, 0)),
        ],
        out_shape=[jax.ShapeDtypeStruct(dx.shape, BF16), jax.ShapeDtypeStruct((d, ff), BF16),
                   jax.ShapeDtypeStruct((d, ff), BF16), jax.ShapeDtypeStruct((ff, d), BF16)],
        compiler_params=pltpu.CompilerParams(vmem_limit_bytes=VMEM_LIMIT, dimension_semantics=("arbitrary",)),
        cost_estimate=pl.CostEstimate(flops=2 * rows * d * ff, bytes_accessed=12 * rows * d, transcendentals=0),
        name="dw_and_results",
    )(yx, act, w, w, dx)


def solution(mesh):
    chips = mesh.shape["tp"] // 2

    def local(x, dy, gate, up, wg, wu, wd):
        yx, act, own, other = call_a(chips, dy, x, gate, up, wd, wg, wu)
        w, dx = call_b(chips, act, yx, own, other)
        return tuple(call_c(act, yx, w, dx))

    rows, cols = P(("dp", "tp"), None), P("dp", "tp")
    return jax.shard_map(local, mesh=mesh,
                         in_specs=(rows, rows, cols, cols, P(None, "tp"), P(None, "tp"), P("tp", None)),
                         out_specs=(rows, cols, cols, P(("dp", "tp"), None)), check_vma=False)
```

time: 442 us -> 290 us (0.66); the launches traced: 435 us -> 290 us
  matrix products: 310 us -> 0 us
  Pallas kernels: 0 us -> 289 us
  waiting for transfers between devices: 86.3 us -> 0 us
  local copies, waits for them, and re-layouts: 24.5 us -> 0 us
  between operations: 14.2 us -> 0.65 us
    dot_general x6 -> x0, matrix products: 310 us -> none  [the longest x3 153 us: by_group(): jnp.einsum('gta,gtb->gab', a, b, preferred_element_type=jnp.float32)]
    pallas_call x0 -> x3, Pallas kernels: none -> 289 us  [the longest x1 152 us: call_a(): pl.pallas_call(functools.partial(kernel_a, chips), grid=(rows // TM,), in...]
    unnamed x5 -> x0, waiting for transfers between devices: 86.2 us -> none
    unnamed x2 -> x0, local copies, waits for them, and re-layouts: 24.5 us -> none
  transfers between devices with their start and end apart: 3 -> 0, of which waited for: 1 -> 0; matrix products, arithmetic and copies ran while one was open for 77% -> 0% of each run, Pallas kernels for 0% -> 0%
where the time goes in v1:
time: 290 us
  Pallas kernels  289 us (100%)
    pallas_call x1, Pallas kernels, call_a(): pl.pallas_call(functools.partial(kernel_a, chips), grid=(rows // TM,), in...  152 us
    pallas_call x1, Pallas kernels, call_b(): pl.pallas_call(functools.partial(kernel_b, chips), grid=(8,), in_specs=[p...  90.5 us
    pallas_call x1, Pallas kernels, call_c(): pl.pallas_call(kernel, grid=(4,), in_specs=[pl.BlockSpec((rows, d // 2),...  46.3 us

profile of v1, /device:TPU:112, one launch (start us, length us, event | category | flops | bytes accessed | tf_op | source)
XLA Modules:
  0.0 290.0 jit_solution(7948246709275321916)
XLA Ops:
  0.6 152.5 %gather_and_dx.1 = (bf16[8192,2048]{1,0:T(8,128)(2,1)}, bf16[4096,6144]{1,0:T(8,128)(2,1)}, f32[2048,2048]{1,0:T(8,128)}, bf16[2048,2048]{1,0:T(8,128)(2,1)}) custom-call(bf16[512,2048]{1,0:T(8,128)(2,1)} %dy_ref.1, bf16[512,2048]{1,0:T(8,128)(2,1)} %x_ref.1, bf16[4096,2048]{1,0:T(8,128)(2,1)} %g_ref.1, bf16[4096,2048]{1,0:T(8,128)(2,1)} %u_ref.1, ...), custom_call_target="tpu_custom_call" | custom-call | flops 103079215104 | bytes 100663296 | tf_op jit(solution)/shard_map/gather_and_dx/pallas_call | solution.py:222
  153.1 90.5 %scatter_and_dw.1 = (bf16[4096,2048]{1,0:T(8,128)(2,1)}, bf16[512,2048]{1,0:T(8,128)(2,1)}) custom-call(bf16[4096,6144]{1,0:T(8,128)(2,1)} %get-tuple-element.11.a_ref.du_ref, bf16[8192,2048]{1,0:T(8,128)(2,1)} %get-tuple-element.10.b_ref.x_ref, f32[2048,2048]{1,0:T(8,128)} %get-tuple-element.12.own_ref, bf16[2048,2048]{1,0:T(8,128)(2,1)} %get-tuple-element.13.other_ref), custom_call_target="tpu_custom_call" | custom-call | flops 68719476736 | bytes 100663296 | tf_op jit(solution)/shard_map/scatter_and_dw/pallas_call | solution.py:344
  243.6 46.3 %dw_and_results.1 = (bf16[512,2048]{1,0:T(8,128)(2,1)}, bf16[2048,2048]{1,0:T(8,128)(2,1)}, bf16[2048,2048]{1,0:T(8,128)(2,1)}, bf16[2048,2048]{1,0:T(8,128)(2,1)}) custom-call(bf16[8192,2048]{1,0:T(8,128)(2,1)} %get-tuple-element.10.b_ref.x_ref, bf16[4096,6144]{1,0:T(8,128)(2,1)} %get-tuple-element.11.a_ref.du_ref, ...), custom_call_target="tpu_custom_call" | custom-call | flops 34359738368 | bytes 100663296 | tf_op jit(solution)/shard_map/dw_and_results/pallas_call | solution.py:382

commit v2 on v1

v2 whole, which is shorter than its diff:
```python
import functools

import jax
import jax.numpy as jnp
from jax import lax
from jax.experimental import pallas as pl
from jax.experimental.pallas import tpu as pltpu
from jax.sharding import PartitionSpec as P

MESH = pl.DeviceIdType.MESH
VMEM_LIMIT = 63 * 2**20
TM = 256
CB = 256
DY_SECOND, DY_FAR, DY_FAR_IN, X_RING, X_FIRST, X_SECOND = 2, 5, 10, (8, 11), 12, 15
F32, BF16 = jnp.float32, jnp.bfloat16
NT = (((1,), (1,)), ((), ()))
TN = (((0,), (0,)), ((), ()))
ROOT, CUBE = 0.7978845608028654, 0.044715


def place(i):
    a = i // 4
    mid, far = ((a + 1) // 2) % 2, a // 3
    chip = mid * (2 * (i % 2) - 1) + 2 * far
    half = mid * ((a - 1 + i % 2) % 2) + (1 - mid) * (i % 2)
    return chip, (i // 2 + far) % 2, half


def row_block(i, chips):
    t = lax.axis_index("tp")
    chip, core, half = place(i)
    return ((((t // 2) + chip + chips) % chips) * 2 + (t % 2 + core) % 2) * 2 + half


def backward_act(dh, g, u):
    g2 = g * g
    t = jnp.tanh(g * (ROOT + (ROOT * CUBE) * g2))
    cdf, rest = 0.5 + 0.5 * t, 0.5 - 0.5 * t
    act = g * cdf
    slope = cdf + act * rest * (2 * ROOT + (6 * ROOT * CUBE) * g2)
    return act * u, dh * u * slope, dh * act


def kernel_a(chips, dy_ref, x_ref, g_ref, u_ref, wd_ref, wg_ref, wu_ref,
             dyf_ref, xf_ref, act_ref, own_ref, other_ref,
             wd, wgu, dybuf, dh, xbuf, sbuf, w_sem, ld_sem, cp_sem, sdy, rdy, sx, rx, so, ro):
    i = pl.program_id(0)
    steps = pl.num_programs(0)
    t = lax.axis_index("tp")
    n = 2 * chips
    partner = t + 1 - 2 * (t % 2)
    right, left = (t + 2) % n, (t + n - 2) % n
    dp = lax.axis_index("dp")
    ff = wd.shape[0]
    tokens = dyf_ref.shape[0]

    def tile(ref, j):
        return ref.at[pl.ds(j * TM, TM)]

    def send(src, full, j, to, ssem, rsem):
        return pltpu.make_async_remote_copy(src_ref=src, dst_ref=tile(full, j), send_sem=ssem.at[j], recv_sem=rsem.at[j],
                                            device_id=(dp, to), device_id_type=MESH)

    def arrived(full, j, ssem, rsem):
        send(tile(full, j), full, j, partner, ssem, rsem).wait_recv()

    def hand_over(j):
        k = (j // 4) * 2 + j % 2
        return send(sbuf.at[j % 2], other_ref, k, partner, so, ro)

    def load(src, slot):
        return pltpu.make_async_copy(src, dybuf.at[slot], ld_sem.at[slot])

    w_copies = [
        pltpu.make_async_copy(wd_ref, wd, w_sem.at[0]),
        pltpu.make_async_copy(wg_ref, wgu.at[:, pl.ds(0, ff)], w_sem.at[1]),
        pltpu.make_async_copy(wu_ref, wgu.at[:, pl.ds(ff, ff)], w_sem.at[2]),
    ]
    x_in = pltpu.make_async_copy(x_ref, xbuf, cp_sem.at[2])
    x_out = pltpu.make_async_copy(xbuf, xf_ref.at[pl.ds(0, 2 * TM)], cp_sem.at[2])

    def put(k):
        return pltpu.make_async_copy(dybuf.at[k], tile(dyf_ref, k), cp_sem.at[k])

    def ring(src, full, ssem, rsem, second):
        send(tile(src, second), full, 4 + 4 * second, right, ssem, rsem).start()
        send(tile(src, 1 - second), full, 5 + 4 * second, left, ssem, rsem).start()

    def pair(src, full, ssem, rsem):
        send(tile(src, 0), full, 2, partner, ssem, rsem).start()
        send(tile(src, 1), full, 3, partner, ssem, rsem).start()

    @pl.when(i == 0)
    def _():
        w_copies[0].start()
        load(tile(dy_ref, 0), 0).start()
        w_copies[1].start()
        w_copies[2].start()
        barrier = pltpu.get_barrier_semaphore()
        for other in (partner, left, right):
            pl.semaphore_signal(barrier, inc=1, device_id=(dp, other), device_id_type=MESH)
        pl.semaphore_wait(barrier, 3)
        pair(dy_ref, dyf_ref, sdy, rdy)
        ring(dy_ref, dyf_ref, sdy, rdy, 0)
        load(tile(dy_ref, 1), 1).start()
        pair(x_ref, xf_ref, sx, rx)

    @pl.when(i == 1)
    def _():
        x_in.start()

    @pl.when(i == 3)
    def _():
        x_in.wait()
        x_out.start()

    @pl.when(i == 5)
    def _():
        x_out.wait()

    j = i + 1

    @pl.when((j >= 2) & (j < 4))
    def _():
        put(j % 2).wait()

    @pl.when((j >= 2) & (j < steps - 2))
    def _():
        arrived(dyf_ref, j, sdy, rdy)

    @pl.when((j >= 2) & (j < steps))
    def _():
        load(tile(dyf_ref, j), j % 2).start()

        @pl.when((j >= 4) & (j < 12) & (j % 4 < 2))
        def _():
            send(tile(dyf_ref, j), dyf_ref, j + 2, partner, sdy, rdy).start()

    @pl.when(i == DY_SECOND)
    def _():
        ring(dy_ref, dyf_ref, sdy, rdy, 1)

    @pl.when(i == DY_FAR)
    def _():
        send(tile(dyf_ref, 4), dyf_ref, 14, right, sdy, rdy).start()
        send(tile(dyf_ref, 5), dyf_ref, 15, left, sdy, rdy).start()

    @pl.when(i == DY_FAR_IN)
    def _():
        for k in (14, 15):
            arrived(dyf_ref, k, sdy, rdy)
            send(tile(dyf_ref, k), dyf_ref, k - 2, partner, sdy, rdy).start()

    for step, second in zip(X_RING, (0, 1)):
        @pl.when(i == step)
        def _(second=second):
            ring(x_ref, xf_ref, sx, rx, second)

    @pl.when((i == X_FIRST) | (i == X_SECOND))
    def _():
        for k in (4, 5):
            k = k + 4 * (i // X_SECOND)
            arrived(xf_ref, k, sx, rx)
            send(tile(xf_ref, k), xf_ref, k + 2, partner, sx, rx).start()

    def for_partner(k):
        return (k >= 0) & ((k // 2 + k // 12) % 2 == 1)

    @pl.when(for_partner(i - 1))
    def _():
        hand_over(i - 1).start()

    @pl.when(for_partner(i - 2))
    def _():
        hand_over(i - 2).wait_send()

    slot = i % 2
    load(tile(dy_ref, 0), slot).wait()

    @pl.when(i < 2)
    def _():
        put(slot).start()

    def first(c):
        cols = pl.ds(pl.multiple_of(c * CB, CB), CB)
        dh[c % 2] = lax.dot_general(dybuf[slot], wd[cols, :], NT, preferred_element_type=F32)
        for r in range(TM // 32):
            part = pl.ds(r * 32, 32)
            values = backward_act(dh[c % 2, part, :], g_ref[part, cols].astype(F32), u_ref[part, cols].astype(F32))
            for k, v in enumerate(values):
                act_ref[part, pl.ds(pl.multiple_of(k * ff + c * CB, CB), CB)] = v.astype(BF16)

    def second(c, width):
        cols = pl.ds(pl.multiple_of(c * width, width), width)
        v = lax.dot_general(act_ref[:, pl.ds(ff, 2 * ff)], wgu[cols, :], NT, preferred_element_type=F32)
        own_ref[:, cols] = v
        sbuf[slot, :, cols] = v.astype(BF16)

    @pl.when(i == 0)
    def _():
        w_copies[0].wait()
        pl.loop(0, ff // CB)(first)
        w_copies[1].wait()
        w_copies[2].wait()
        pl.loop(0, wgu.shape[0] // 512)(lambda c: second(c, 512))

    @pl.when(i > 0)
    def _():
        for c in range(ff // CB):
            first(c)
        second(0, wgu.shape[0])

    @pl.when(i == steps - 1)
    def _():
        for k in (2, 3, 6, 7, 10, 11):
            arrived(xf_ref, k, sx, rx)
        for k in range(2, 16):
            send(tile(dy_ref, 0), dyf_ref, k, partner, sdy, rdy).wait_send()
        for k in range(2, 12):
            send(tile(x_ref, 0), xf_ref, k, partner, sx, rx).wait_send()
        for k in range(tokens // TM // 2):
            send(sbuf.at[0], other_ref, k, partner, so, ro).wait_recv()


def call_a(chips, dy, x, gate, up, wd, wg, wu):
    rows, ff = gate.shape
    d = dy.shape[1]
    any_ = pl.BlockSpec(memory_space=pl.ANY)
    kept = pl.BlockSpec((TM, ff), lambda i: (row_block(i, chips), 0))
    return pl.pallas_call(
        functools.partial(kernel_a, chips),
        grid=(rows // TM,),
        in_specs=[any_, any_, kept, kept, any_, any_, any_],
        out_specs=[
            any_, any_,
            pl.BlockSpec((TM, 3 * ff), lambda i: (i, 0)),
            pl.BlockSpec((TM, d), lambda i: (i, 0)),
            any_,
        ],
        out_shape=[
            jax.ShapeDtypeStruct((rows, d), BF16), jax.ShapeDtypeStruct((rows * 3 // 4, d), BF16),
            jax.ShapeDtypeStruct((rows, 3 * ff), BF16),
            jax.ShapeDtypeStruct((rows, d), F32), jax.ShapeDtypeStruct((rows // 2, d), BF16),
        ],
        scratch_shapes=[
            pltpu.VMEM((ff, d), BF16), pltpu.VMEM((d, 2 * ff), BF16),
            pltpu.VMEM((2, TM, d), BF16), pltpu.VMEM((2, TM, CB), F32), pltpu.VMEM((2 * TM, d), BF16), pltpu.VMEM((2, TM, d), BF16),
            pltpu.SemaphoreType.DMA((3,)), pltpu.SemaphoreType.DMA((2,)), pltpu.SemaphoreType.DMA((3,)),
            pltpu.SemaphoreType.DMA((16,)), pltpu.SemaphoreType.DMA((16,)),
            pltpu.SemaphoreType.DMA((16,)), pltpu.SemaphoreType.DMA((16,)),
            pltpu.SemaphoreType.DMA((8,)), pltpu.SemaphoreType.DMA((8,)),
        ],
        compiler_params=pltpu.CompilerParams(collective_id=0, has_side_effects=True, vmem_limit_bytes=VMEM_LIMIT,
                                             dimension_semantics=("arbitrary",)),
        cost_estimate=pl.CostEstimate(flops=6 * rows * d * ff, bytes_accessed=12 * rows * d, transcendentals=rows * ff),
        name="gather_and_dx",
    )(dy, x, gate, up, wd, wg, wu)


SUB = TM // 2
HOPS = ((4, 14, 9, 0), (5, 15, 8, 1))
FAR_STEP = 3


def kernel_b(chips, a_ref, dyf_ref, xn_ref, own_ref, other_ref, w_ref, dx_ref, xfar_ref,
             b_buf, own, other, come, go, b_sem, ld_sem, s_sem, r_sem, o_sem, sf, rf):
    s = pl.program_id(0)
    last = pl.num_programs(0) - 1
    t = lax.axis_index("tp")
    n = 2 * chips
    dp = lax.axis_index("dp")
    partner = t + 1 - 2 * (t % 2)
    ways = ((t + 2) % n, (t + n - 2) % n)
    near = xn_ref.shape[0]
    half_d = b_buf.shape[2]

    def fetch_dy(k):
        cols = pl.ds(pl.multiple_of((k % 2) * half_d, half_d), half_d)
        return pltpu.make_async_copy(dyf_ref.at[:, cols], b_buf.at[k % 2], b_sem.at[k % 2, 0])

    def fetch_near(k):
        cols = pl.ds(pl.multiple_of((k % 2) * half_d, half_d), half_d)
        return pltpu.make_async_copy(xn_ref.at[:, cols], b_buf.at[k % 2, pl.ds(0, near)], b_sem.at[k % 2, 0])

    def fetch_far(k):
        cols = pl.ds(pl.multiple_of((k % 2) * half_d, half_d), half_d)
        far = b_buf.shape[1] - near
        return pltpu.make_async_copy(xfar_ref.at[:, cols], b_buf.at[k % 2, pl.ds(near, far)], b_sem.at[k % 2, 1])

    def fetch_x(k):
        return fetch_near(k), fetch_far(k)

    def far_send(k):
        src = xn_ref.at[pl.ds((4 + k) * TM, TM)] if k < 2 else xfar_ref.at[pl.ds(k * TM, TM)]
        to = ways[k] if k < 2 else partner
        return pltpu.make_async_remote_copy(src_ref=src, dst_ref=xfar_ref.at[pl.ds((k + 2) % 4 * TM, TM)], send_sem=sf.at[k],
                                            recv_sem=rf.at[k], device_id=(dp, to), device_id_type=MESH)

    def joins(w, h):
        odd, high = h % 2, h // 2
        k0, k1, k2, k3 = HOPS[w]
        return (1 - odd) * (1 - high) * k0 + odd * (1 - high) * k1 + (1 - odd) * high * k2 + odd * high * k3

    def loads(e):
        for w in range(2):
            k = joins(w, e // 2)
            at = pl.ds(pl.multiple_of(k * TM + (e % 2) * SUB, SUB), SUB)
            yield pltpu.make_async_copy(own_ref.at[at], own.at[e % 2, w], ld_sem.at[e % 2, w, 0])
            at = pl.ds(pl.multiple_of(((k // 4) * 2 + k % 2) * TM + (e % 2) * SUB, SUB), SUB)
            yield pltpu.make_async_copy(other_ref.at[at], other.at[e % 2, w], ld_sem.at[e % 2, w, 1])

    def send(e, w):
        return pltpu.make_async_remote_copy(src_ref=go.at[e % 2, w], dst_ref=come.at[e, w], send_sem=s_sem.at[e, w],
                                            recv_sem=r_sem.at[e, w], device_id=(dp, ways[w]), device_id_type=MESH)

    def finish(e, w):
        at = pl.ds(pl.multiple_of(w * TM + (e % 2) * SUB, SUB), SUB)
        return pltpu.make_async_copy(go.at[e % 2, w], dx_ref.at[at], o_sem.at[e % 2, w])

    def add(e, carried):
        for w in range(2):
            for r in range(SUB // 16):
                rows = pl.ds(r * 16, 16)
                v = own[e % 2, w, rows, :] + other[e % 2, w, rows, :].astype(F32)
                if carried:
                    v = v + come[e - 2, w, rows, :].astype(F32)
                go[e % 2, w, rows, :] = v.astype(BF16)

    def event(e):
        for c in loads(e):
            c.wait()

        @pl.when(e < 7)
        def _():
            for c in loads(e + 1):
                c.start()

        @pl.when(e < 2)
        def _():
            add(e, False)

        @pl.when(e >= 2)
        def _():
            for w in range(2):
                send(e - 2, w).wait_recv()
                send(e - 2, w).wait_send()
            add(e, True)

        @pl.when(e < 6)
        def _():
            for w in range(2):
                send(e, w).start()

        @pl.when(e >= 6)
        def _():
            for w in range(2):
                finish(e, w).start()

    @pl.when(s == 0)
    def _():
        fetch_dy(0).start()
        for c in loads(0):
            c.start()
        barrier = pltpu.get_barrier_semaphore()
        for peer in (partner, *ways):
            pl.semaphore_signal(barrier, inc=1, device_id=(dp, peer), device_id_type=MESH)
        pl.semaphore_wait(barrier, 3)
        for k in (0, 1):
            far_send(k).start()
        fetch_dy(0).wait()

    @pl.when((s > 0) & (s < 4))
    def _():
        fetch_dy(s).wait()

    @pl.when(s == FAR_STEP + 1)
    def _():
        for k in (2, 3):
            far_send(k).wait_recv()
        fetch_far(s).start()

    @pl.when((s >= 4) & (s < last))
    def _():
        for c in fetch_x(s):
            c.wait()

    @pl.when(s < 3)
    def _():
        fetch_dy(s + 1).start()

    @pl.when(s == FAR_STEP)
    def _():
        for k in (0, 1):
            far_send(k).wait_recv()
            far_send(k + 2).start()
        fetch_near(s + 1).start()

    @pl.when((s > FAR_STEP) & (s < last - 1))
    def _():
        for c in fetch_x(s + 1):
            c.start()

    @pl.when((s > 0) & (s % 4 < 3))
    def _():
        event(s - 1 - s // 4)

    slot = s % 2

    @pl.when(s < 4)
    def _():
        w_ref[...] = lax.dot_general(a_ref[...], b_buf[slot], TN, preferred_element_type=F32).astype(BF16)

    @pl.when((s >= 4) & (s < last))
    def _():
        w_ref[...] = lax.dot_general(b_buf[slot], a_ref[...], TN, preferred_element_type=F32).astype(BF16)

    @pl.when(s == last)
    def _():
        for k in range(4):
            far_send(k).wait_send()
        for e in (6, 7):
            for w in range(2):
                finish(e, w).wait()


def call_b(chips, act, dyf, xn, own, other):
    rows, d = dyf.shape
    ff = act.shape[1] // 3
    any_ = pl.BlockSpec(memory_space=pl.ANY)
    x_part = lambda s: jnp.minimum(s // 4, 1)

    def block(s):
        s = jnp.minimum(s, 9)
        x = x_part(s)
        return (1 - x) * (s // 2) + x * (2 * (s // 4) + s % 2), (1 - x) * (s % 2) + x * ((s // 2) % 2)

    return pl.pallas_call(
        functools.partial(kernel_b, chips),
        grid=(11,),
        in_specs=[pl.BlockSpec((rows, ff // 2), lambda s: (0, jnp.minimum(s, 9) // 2)), any_, any_, any_, any_],
        out_specs=[pl.BlockSpec((d // 2, d // 2), block), any_, any_],
        out_shape=[jax.ShapeDtypeStruct((ff + 2 * d, d), BF16), jax.ShapeDtypeStruct((2 * TM, d), BF16),
                   jax.ShapeDtypeStruct((rows // 4, d), BF16)],
        scratch_shapes=[
            pltpu.VMEM((2, rows, d // 2), BF16),
            pltpu.VMEM((2, 2, SUB, d), F32), pltpu.VMEM((2, 2, SUB, d), BF16),
            pltpu.VMEM((6, 2, SUB, d), BF16), pltpu.VMEM((2, 2, SUB, d), BF16),
            pltpu.SemaphoreType.DMA((2, 2)),
            pltpu.SemaphoreType.DMA((2, 2, 2)), pltpu.SemaphoreType.DMA((6, 2)), pltpu.SemaphoreType.DMA((6, 2)),
            pltpu.SemaphoreType.DMA((2, 2)), pltpu.SemaphoreType.DMA((4,)), pltpu.SemaphoreType.DMA((4,)),
        ],
        compiler_params=pltpu.CompilerParams(collective_id=1, has_side_effects=True, vmem_limit_bytes=VMEM_LIMIT,
                                             dimension_semantics=("arbitrary",)),
        cost_estimate=pl.CostEstimate(flops=5 * rows * d * ff, bytes_accessed=12 * rows * d, transcendentals=0),
        name="scatter_and_dw",
    )(act, dyf, xn, own, other)


def call_c(act, xn, xfar, w, dx):
    rows, d = act.shape[0], xn.shape[1]
    ff = act.shape[1] // 3
    near = xn.shape[0]
    cut = 4

    def kernel(xn_ref, xfar_ref, du_ref, wd_ref, wg_ref, wu_ref, dx_ref, dx_out, wg_out, wu_out, wd_out):
        dx_out[...] = dx_ref[...]
        wg_out[...] = wg_ref[...]
        wd_out[...] = wd_ref[...]
        wu_out[:, :ff // 2] = wu_ref[...]
        v = lax.dot_general(xn_ref[...], du_ref[:near], TN, preferred_element_type=F32)
        v = v + lax.dot_general(xfar_ref[...], du_ref[near:], TN, preferred_element_type=F32)
        wu_out[:, ff // 2:] = v.astype(BF16)

    rows_of = lambda size, start=0: pl.BlockSpec((size // cut, d), lambda s: (start + s, 0))
    return pl.pallas_call(
        kernel,
        grid=(cut,),
        in_specs=[
            pl.BlockSpec((near, d // cut), lambda s: (0, s)),
            pl.BlockSpec((rows - near, d // cut), lambda s: (0, s)),
            pl.BlockSpec((rows, ff // 2), lambda s: (0, 5)),
            rows_of(ff), rows_of(d, cut),
            pl.BlockSpec((d // cut, ff // 2), lambda s: (2 * cut + s, 0)),
            rows_of(dx.shape[0]),
        ],
        out_specs=[rows_of(dx.shape[0]), rows_of(d), rows_of(d), rows_of(ff)],
        out_shape=[jax.ShapeDtypeStruct(dx.shape, BF16), jax.ShapeDtypeStruct((d, ff), BF16),
                   jax.ShapeDtypeStruct((d, ff), BF16), jax.ShapeDtypeStruct((ff, d), BF16)],
        compiler_params=pltpu.CompilerParams(vmem_limit_bytes=VMEM_LIMIT, dimension_semantics=("arbitrary",)),
        cost_estimate=pl.CostEstimate(flops=rows * d * ff, bytes_accessed=12 * rows * d, transcendentals=0),
        name="dw_and_results",
    )(xn, xfar, act, w, w, w, dx)


def solution(mesh):
    chips = mesh.shape["tp"] // 2

    def local(x, dy, gate, up, wg, wu, wd):
        dyf, xn, act, own, other = call_a(chips, dy, x, gate, up, wd, wg, wu)
        w, dx, xfar = call_b(chips, act, dyf, xn, own, other)
        return tuple(call_c(act, xn, xfar, w, dx))

    rows, cols = P(("dp", "tp"), None), P("dp", "tp")
    return jax.shard_map(local, mesh=mesh,
                         in_specs=(rows, rows, cols, cols, P(None, "tp"), P(None, "tp"), P("tp", None)),
                         out_specs=(rows, cols, cols, P(("dp", "tp"), None)), check_vma=False)
```

time: 290 us -> 274 us (0.945)
  Pallas kernels: 289 us -> 273 us
    pallas_call x1, Pallas kernels: 152 us -> 135 us  [call_a(): pl.pallas_call(functools.partial(kernel_a, chips), grid=(rows // TM,), in...]
where the time goes in v2:
time: 274 us; the launch traced here: 273 us
  Pallas kernels  273 us (100%)
    pallas_call x1, Pallas kernels, call_a(): pl.pallas_call(functools.partial(kernel_a, chips), grid=(rows // TM,), in...  135 us
    pallas_call x1, Pallas kernels, call_b(): pl.pallas_call(functools.partial(kernel_b, chips), grid=(11,), in_specs=[...  106 us
    pallas_call x1, Pallas kernels, call_c(): pl.pallas_call(kernel, grid=(cut,), in_specs=[pl.BlockSpec((near, d // cu...  31.6 us

profile of v2, /device:TPU:112, one launch (start us, length us, event | category | flops | bytes accessed | tf_op | source)
XLA Modules:
  0.0 273.4 jit_solution(7246064320690707107)
XLA Ops:
  0.6 134.9 %gather_and_dx.1 = (bf16[4096,2048]{1,0:T(8,128)(2,1)}, bf16[3072,2048]{1,0:T(8,128)(2,1)}, bf16[4096,6144]{1,0:T(8,128)(2,1)}, f32[4096,2048]{1,0:T(8,128)}, bf16[2048,2048]{1,0:T(8,128)(2,1)}) custom-call(bf16[512,2048]{1,0:T(8,128)(2,1)} %dy_ref.1, bf16[512,2048]{1,0:T(8,128)(2,1)} %x_ref.1, bf16[4096,2048]{1,0:T(8,128)(2,1)} %g_ref.1, ...), custom_call_target="tpu_custom_call" | custom-call | flops 103079215104 | bytes 100663296 | tf_op jit(solution)/shard_map/gather_and_dx/pallas_call | solution.py:230
  135.5 106.2 %scatter_and_dw.1 = (bf16[6144,2048]{1,0:T(8,128)(2,1)}, bf16[512,2048]{1,0:T(8,128)(2,1)}, bf16[1024,2048]{1,0:T(8,128)(2,1)}) custom-call(bf16[4096,6144]{1,0:T(8,128)(2,1)} %get-tuple-element.13.a_ref.du_ref, bf16[4096,2048]{1,0:T(8,128)(2,1)} %get-tuple-element.14.dyf_ref, bf16[3072,2048]{1,0:T(8,128)(2,1)} %get-tuple-element.12.xn_ref, ...), custom_call_target="tpu_custom_call" | custom-call | flops 85899345920 | bytes 100663296 | tf_op jit(solution)/shard_map/scatter_and_dw/pallas_call | solution.py:437
  241.7 31.6 %dw_and_results.1 = (bf16[512,2048]{1,0:T(8,128)(2,1)}, bf16[2048,2048]{1,0:T(8,128)(2,1)}, bf16[2048,2048]{1,0:T(8,128)(2,1)}, bf16[2048,2048]{1,0:T(8,128)(2,1)}) custom-call(bf16[3072,2048]{1,0:T(8,128)(2,1)} %get-tuple-element.12.xn_ref, bf16[1024,2048]{1,0:T(8,128)(2,1)} %get-tuple-element.17.xfar_ref, ...), custom_call_target="tpu_custom_call" | custom-call | flops 17179869184 | bytes 100663296 | tf_op jit(solution)/shard_map/dw_and_results/pallas_call | solution.py:475

commit v3 on v2

--- a/solution.py
+++ b/solution.py
@@ -10,7 +10,7 @@
 MESH = pl.DeviceIdType.MESH
 VMEM_LIMIT = 63 * 2**20
 TM = 256
-CB = 256
+CB, NB = 256, 512
 DY_SECOND, DY_FAR, DY_FAR_IN, X_RING, X_FIRST, X_SECOND = 2, 5, 10, (8, 11), 12, 15
 F32, BF16 = jnp.float32, jnp.bfloat16
 NT = (((1,), (1,)), ((), ()))
@@ -71,11 +71,15 @@
     def load(src, slot):
         return pltpu.make_async_copy(src, dybuf.at[slot], ld_sem.at[slot])
 
-    w_copies = [
-        pltpu.make_async_copy(wd_ref, wd, w_sem.at[0]),
-        pltpu.make_async_copy(wg_ref, wgu.at[:, pl.ds(0, ff)], w_sem.at[1]),
-        pltpu.make_async_copy(wu_ref, wgu.at[:, pl.ds(ff, ff)], w_sem.at[2]),
-    ]
+    def load_down(c):
+        at = pl.ds(pl.multiple_of(c * CB, CB), CB)
+        return pltpu.make_async_copy(wd_ref.at[at], wd.at[at], w_sem.at[0, c])
+
+    def load_gate_up(c):
+        at = pl.ds(pl.multiple_of(c * NB, NB), NB)
+        return (pltpu.make_async_copy(wg_ref.at[at], wgu.at[at, pl.ds(0, ff)], w_sem.at[1, c]),
+                pltpu.make_async_copy(wu_ref.at[at], wgu.at[at, pl.ds(ff, ff)], w_sem.at[2, c]))
+
     x_in = pltpu.make_async_copy(x_ref, xbuf, cp_sem.at[2])
     x_out = pltpu.make_async_copy(xbuf, xf_ref.at[pl.ds(0, 2 * TM)], cp_sem.at[2])
 
@@ -92,10 +96,14 @@
 
     @pl.when(i == 0)
     def _():
-        w_copies[0].start()
         load(tile(dy_ref, 0), 0).start()
-        w_copies[1].start()
-        w_copies[2].start()
+        pl.loop(0, ff // CB)(lambda c: load_down(c).start())
+
+        @pl.loop(0, wgu.shape[0] // NB)
+        def _(c):
+            for copy in load_gate_up(c):
+                copy.start()
+
         barrier = pltpu.get_barrier_semaphore()
         for other in (partner, left, right):
             pl.semaphore_signal(barrier, inc=1, device_id=(dp, other), device_id_type=MESH)
@@ -198,11 +206,16 @@
 
     @pl.when(i == 0)
     def _():
-        w_copies[0].wait()
-        pl.loop(0, ff // CB)(first)
-        w_copies[1].wait()
-        w_copies[2].wait()
-        pl.loop(0, wgu.shape[0] // 512)(lambda c: second(c, 512))
+        @pl.loop(0, ff // CB)
+        def _(c):
+            load_down(c).wait()
+            first(c)
+
+        @pl.loop(0, wgu.shape[0] // NB)
+        def _(c):
+            for copy in load_gate_up(c):
+                copy.wait()
+            second(c, NB)
 
     @pl.when(i > 0)
     def _():
@@ -245,7 +258,7 @@
         scratch_shapes=[
             pltpu.VMEM((ff, d), BF16), pltpu.VMEM((d, 2 * ff), BF16),
             pltpu.VMEM((2, TM, d), BF16), pltpu.VMEM((2, TM, CB), F32), pltpu.VMEM((2 * TM, d), BF16), pltpu.VMEM((2, TM, d), BF16),
-            pltpu.SemaphoreType.DMA((3,)), pltpu.SemaphoreType.DMA((2,)), pltpu.SemaphoreType.DMA((3,)),
+            pltpu.SemaphoreType.DMA((3, 8)), pltpu.SemaphoreType.DMA((2,)), pltpu.SemaphoreType.DMA((3,)),
             pltpu.SemaphoreType.DMA((16,)), pltpu.SemaphoreType.DMA((16,)),
             pltpu.SemaphoreType.DMA((16,)), pltpu.SemaphoreType.DMA((16,)),
             pltpu.SemaphoreType.DMA((8,)), pltpu.SemaphoreType.DMA((8,)),
@@ -460,7 +473,7 @@
     rows, d = act.shape[0], xn.shape[1]
     ff = act.shape[1] // 3
     near = xn.shape[0]
-    cut = 4
+    cut = 8
 
     def kernel(xn_ref, xfar_ref, du_ref, wd_ref, wg_ref, wu_ref, dx_ref, dx_out, wg_out, wu_out, wd_out):
         dx_out[...] = dx_ref[...]

time: 274 us -> 271 us (0.989)
  Pallas kernels: 273 us -> 270 us
where the time goes in v3:
time: 271 us
  Pallas kernels  270 us (100%)
    pallas_call x1, Pallas kernels, call_a(): pl.pallas_call(functools.partial(kernel_a, chips), grid=(rows // TM,), in...  133 us
    pallas_call x1, Pallas kernels, call_b(): pl.pallas_call(functools.partial(kernel_b, chips), grid=(11,), in_specs=[...  106 us
    pallas_call x1, Pallas kernels, call_c(): pl.pallas_call(kernel, grid=(cut,), in_specs=[pl.BlockSpec((near, d // cu...  31.5 us

profile of v3, /device:TPU:112, one launch (start us, length us, event | category | flops | bytes accessed | tf_op | source)
XLA Modules:
  0.0 270.7 jit_solution(11681183192821788877)
XLA Ops:
  0.6 132.8 %gather_and_dx.1 = (bf16[4096,2048]{1,0:T(8,128)(2,1)}, bf16[3072,2048]{1,0:T(8,128)(2,1)}, bf16[4096,6144]{1,0:T(8,128)(2,1)}, f32[4096,2048]{1,0:T(8,128)}, bf16[2048,2048]{1,0:T(8,128)(2,1)}) custom-call(bf16[512,2048]{1,0:T(8,128)(2,1)} %dy_ref.1, bf16[512,2048]{1,0:T(8,128)(2,1)} %x_ref.1, bf16[4096,2048]{1,0:T(8,128)(2,1)} %g_ref.1, ...), custom_call_target="tpu_custom_call" | custom-call | flops 103079215104 | bytes 100663296 | tf_op jit(solution)/shard_map/gather_and_dx/pallas_call | solution.py:243
  133.4 105.8 %scatter_and_dw.1 = (bf16[6144,2048]{1,0:T(8,128)(2,1)}, bf16[512,2048]{1,0:T(8,128)(2,1)}, bf16[1024,2048]{1,0:T(8,128)(2,1)}) custom-call(bf16[4096,6144]{1,0:T(8,128)(2,1)} %get-tuple-element.13.a_ref.du_ref, bf16[4096,2048]{1,0:T(8,128)(2,1)} %get-tuple-element.14.dyf_ref, bf16[3072,2048]{1,0:T(8,128)(2,1)} %get-tuple-element.12.xn_ref, ...), custom_call_target="tpu_custom_call" | custom-call | flops 85899345920 | bytes 100663296 | tf_op jit(solution)/shard_map/scatter_and_dw/pallas_call | solution.py:450
  239.2 31.5 %dw_and_results.1 = (bf16[512,2048]{1,0:T(8,128)(2,1)}, bf16[2048,2048]{1,0:T(8,128)(2,1)}, bf16[2048,2048]{1,0:T(8,128)(2,1)}, bf16[2048,2048]{1,0:T(8,128)(2,1)}) custom-call(bf16[3072,2048]{1,0:T(8,128)(2,1)} %get-tuple-element.12.xn_ref, bf16[1024,2048]{1,0:T(8,128)(2,1)} %get-tuple-element.17.xfar_ref, ...), custom_call_target="tpu_custom_call" | custom-call | flops 17179869184 | bytes 100663296 | tf_op jit(solution)/shard_map/dw_and_results/pallas_call | solution.py:488
